TPU v7x, 256 devices: a whole 4x4x8 slice. The times are simulated.
256 devices in a mesh: section: 8 (over y_hi, x), tensor: 16 (over z, core), dp: 2 (over y_lo).
Axes of the slice: x: 4, y: 4 (y_hi: 2, y_lo: 2; y = y_hi * 2 + y_lo), z: 8, core: 2. Of those that a mesh axis runs over, the one named last changes fastest.
Arguments:
- dec_queries: bfloat16 [8, 4, 512, 16384], P('section', 'dp', None, 'tensor'), may hold values from -8 to 8
- enc_keys: bfloat16 [8, 4, 512, 16384], P('section', 'dp', None, 'tensor'), may hold values from -4 to 4
- enc_values: bfloat16 [8, 4, 512, 16384], P('section', 'dp', None, 'tensor'), may hold values from -4 to 4
- out_grad: bfloat16 [8, 4, 512, 16384], P('section', 'dp', None, 'tensor'), may hold values from -15 to 15
- key_weight: bfloat16 [8, 1024, 16384], P('section', None, 'tensor'), may hold values from -0.1875 to 0.1875
- value_weight: bfloat16 [8, 1024, 16384], P('section', None, 'tensor'), may hold values from -0.1875 to 0.1875
- enc_hidden: float32 [4, 512, 1024], P('dp', 'section', 'tensor'), may hold values from -2 to 2, as said below
- enc_gain: float32 [1024], P('tensor'), may hold values from 0.1 to 1.9
Outputs:
- enc_input_grad: float32 [4, 512, 1024], P('dp', 'section', 'tensor')
Inputs may be any that keep to these rules, and one draw needn't show every extreme that they name: `enc_hidden`: every entry's magnitude is at least 0.25.
All inputs are finite; a program needn't handle non-finite values.
Results may differ from a plain program's by a relative error of at most 0.0041.
Values sent between devices are 32-bit elements; how exact they have to be, the bound alone decides.
A program may use at most 128 MiB of HBM per device.

v0:
```python
import jax
import jax.numpy as jnp
from jax import lax
from jax.sharding import PartitionSpec as P

D = 1024
DK = 128


epsilon = 1e-06


def in_blocks(shard, dim, peers):
    before, after = (shard.shape[:dim], shard.shape[dim + 1 :])
    return jnp.moveaxis(shard.reshape(*before, peers, -1, *after), dim, 0)


def sent_and_summed(shard, axis, dim):
    peers = lax.axis_size(axis)
    blocks = lax.all_to_all(in_blocks(shard, dim, peers), axis, 0, 0, tiled=True)
    return jnp.sum(blocks, axis=0)


def from_everyone(shard, axis):
    copies = jnp.broadcast_to(shard, (lax.axis_size(axis), *shard.shape))
    return lax.all_to_all(copies, axis, split_axis=0, concat_axis=0, tiled=True)


def of_everyone(shard, axis):
    return from_everyone(shard, axis).sum(axis=0)


def in_one(arrays, axis):
    ravelled, at, finished = (jnp.concatenate([a.reshape(-1) for a in arrays]), 0, [])
    subtotal = of_everyone(ravelled, axis)
    for a in arrays:
        finished.append(subtotal[at : at + a.size].reshape(a.shape))
        at += a.size
    return tuple(finished)


def per_device(
    dec_queries, enc_keys, enc_values, out_grad, key_weight, value_weight, enc_hidden, enc_gain
):
    seqs_here = dec_queries.shape[1]
    dec_len = dec_queries.shape[2]
    hidden_here = dec_queries.shape[3]
    enc_len = enc_keys.shape[2]
    heads_here = hidden_here // DK
    model_width = key_weight.shape[1]
    query_heads = dec_queries[0].reshape(seqs_here, dec_len, heads_here, DK)
    key_heads = enc_keys[0].reshape(seqs_here, enc_len, heads_here, DK)
    value_heads = enc_values[0].reshape(seqs_here, enc_len, heads_here, DK)
    grad_heads = out_grad[0].reshape(seqs_here, dec_len, heads_here, DK)
    scores = jnp.einsum(
        "bqhd,bkhd->bhqk", query_heads, key_heads, preferred_element_type=jnp.float32
    )
    shifted = jnp.exp(scores - jnp.max(scores, axis=-1, keepdims=True))
    attn_probs = shifted / jnp.sum(shifted, axis=-1, keepdims=True)
    probs_low = attn_probs.astype(jnp.bfloat16)
    attended = jnp.einsum(
        "bhqk,bkhd->bqhd", probs_low, value_heads, preferred_element_type=jnp.float32
    )
    row_dot = jnp.sum(grad_heads.astype(jnp.float32) * attended, axis=-1)
    value_grad = jnp.einsum(
        "bhqk,bqhd->bkhd", probs_low, grad_heads, preferred_element_type=jnp.float32
    ).astype(jnp.bfloat16)
    prob_grad = jnp.einsum(
        "bqhd,bkhd->bhqk", grad_heads, value_heads, preferred_element_type=jnp.float32
    )
    score_low = (attn_probs * (prob_grad - jnp.transpose(row_dot, (0, 2, 1))[..., None])).astype(
        jnp.bfloat16
    )
    key_grad = jnp.einsum(
        "bhqk,bqhd->bkhd", score_low, query_heads, preferred_element_type=jnp.float32
    ).astype(jnp.bfloat16)
    flat_rows = seqs_here * enc_len
    partial_value = jnp.einsum(
        "th,dh->td",
        key_grad.reshape(flat_rows, hidden_here),
        key_weight[0],
        preferred_element_type=jnp.float32,
    )
    partial_value = partial_value + jnp.einsum(
        "th,dh->td",
        value_grad.reshape(flat_rows, hidden_here),
        value_weight[0],
        preferred_element_type=jnp.float32,
    )
    partial_value = partial_value.reshape(seqs_here, enc_len, model_width)
    layer_part = lax.psum_scatter(partial_value, "section", scatter_dimension=1, tiled=True)
    enc_grad = sent_and_summed(layer_part, "tensor", 2)
    scaled = enc_gain * enc_grad
    cross_local = jnp.sum(scaled * enc_hidden, axis=-1)
    square_total, cross_total = in_one(
        (jnp.sum(enc_hidden * enc_hidden, axis=-1), cross_local), "tensor"
    )
    inverse = lax.rsqrt(square_total / D + epsilon)
    return (
        scaled * inverse[..., None]
        - enc_hidden * (cross_total * inverse * inverse * inverse / D)[..., None]
    )


def solution(mesh):
    return jax.shard_map(
        per_device,
        mesh=mesh,
        in_specs=(
            P("section", "dp", None, "tensor"),
            P("section", "dp", None, "tensor"),
            P("section", "dp", None, "tensor"),
            P("section", "dp", None, "tensor"),
            P("section", None, "tensor"),
            P("section", None, "tensor"),
            P("dp", "section", "tensor"),
            P("tensor"),
        ),
        out_specs=P("dp", "section", "tensor"),
        check_vma=False,
    )
```

profile of v0, /device:TPU:1, one launch (start us, length us, event | category | flops | bytes accessed | tf_op | source)
XLA Modules:
  0.0 212.0 jit_solution(7132976229165001363)
XLA Ops:
  6.5 0.0 copy-start
  6.5 0.0 reduce-scatter.2.cloned.1.call-start
  6.5 0.0 copy-start.3
  6.5 3.7 %copy.89 = bf16[128,8,8,128]{3,2,1,0:T(8,128)(2,1)} copy(bf16[128,8,8,128]{3,1,2,0:T(8,128)(2,1)} %bitcast.57) | data formatting | bytes 4194304
  10.3 0.0 copy-done.3
  10.3 2.0 copy.90
  12.2 3.9 %copy.65 = bf16[1,2,512,1024]{2,3,1,0:T(8,128)(2,1)} copy(bf16[1,2,512,1024]{3,2,1,0:T(8,128)(2,1)} %param.11) | data formatting | bytes 4194304 | tf_op args[3]
  16.2 3.9 %copy.88 = bf16[1,2,512,1024]{2,3,1,0:T(8,128)(2,1)} copy(bf16[1,2,512,1024]{3,2,1,0:T(8,128)(2,1)} %param.10) | data formatting | bytes 4194304 | tf_op jit(solution)/shard_map/reshape;squeeze | solution.py:53
  20.1 10.7 %fusion.30 = (f32[2,8,512]{2,1,0:T(8,128)S(1)}, f32[2,8,512,512]{2,3,1,0:T(8,128)}) fusion(bf16[2,512,8,128]{3,2,1,0:T(8,128)(2,1)} %bitcast.62, bf16[2,512,8,128]{3,2,1,0:T(8,128)(2,1)} %bitcast.59), kind=kOutput, calls=%fused_computation.33 | convolution fusion | flops 1082130944 | bytes 21004288 | tf_op jit(solution)/shard_map/sub | solution.py:58
  30.8 0.0 copy-start.1
  30.8 6.8 %fusion.3 = bf16[2,8,512,512]{2,3,1,0:T(8,128)(2,1)S(1)} fusion(f32[2,8,512,512]{2,3,1,0:T(8,128)} %get-tuple-element.10, f32[2,8,512]{2,1,0:T(8,128)S(1)} %get-tuple-element.9), kind=kLoop, calls=%fused_computation.6 | loop fusion | flops 8388608 | bytes 25198592 | tf_op jit(solution)/shard_map/convert_element_type | solution.py:60
  37.7 0.0 copy-done.1
  37.7 0.0 copy-start.2
  37.7 3.7 %convert_bitcast_fusion = bf16[2,512,8,128]{3,1,2,0:T(8,128)(2,1)} fusion(bf16[2,8,512,512]{2,3,1,0:T(8,128)(2,1)S(1)} %fusion.3, bf16[2,512,8,128]{1,3,2,0:T(8,128)(2,1)S(1)} %bitcast.51), kind=kOutput, calls=%fused_computation.20 | convolution fusion | flops 1074790400 | bytes 12582912 | tf_op jit(solution)/shard_map/bhqk,bqhd->bkhd/dot_general | solution.py:65
  41.3 0.0 copy-done.2
  41.3 1.3 fusion.6
  42.6 11.6 %convert_bitcast_fusion.1 = bf16[2,512,8,128]{3,1,2,0:T(8,128)(2,1)} fusion(f32[2,8,512]{2,1,0:T(8,128)S(1)} %bitcast.64, f32[2,8,512,512]{2,3,1,0:T(8,128)} %get-tuple-element.10, f32[2,8,512]{2,1,0:T(8,128)S(1)} %get-tuple-element.9, bf16[2,512,8,128]{1,3,2,0:T(8,128)(2,1)} %bitcast.53, bf16[2,512,8,128]{1,3,2,0:T(8,128)(2,1)} %bitcast.50, ...), kind=kOutput, calls=%fused_computation.21 | convolution fusion | flops 2165309440 | bytes 25231360 | tf_op jit(solution)/shard_map/bhqk,bqhd->bkhd/dot_general | solution.py:74
  54.2 0.0 copy-start.4
  54.2 3.1 %copy.74 = bf16[2,512,8,128]{3,2,1,0:T(8,128)(2,1)S(1)} copy(bf16[2,512,8,128]{3,1,2,0:T(8,128)(2,1)} %convert_bitcast_fusion.1) | data formatting | bytes 4194304 | tf_op jit(solution)/shard_map/convert_element_type | solution.py:76
  57.3 0.0 copy-done.4
  57.3 1.4 copy.76
  58.7 0.0 copy-done
  58.7 0.0 copy-start.7
  58.7 2.4 %fusion.7 = f32[1024,1024]{1,0:T(8,128)S(1)} fusion(bf16[128,8,8,128]{3,2,1,0:T(8,128)(2,1)S(1)} %bitcast.63, bf16[1,1024,1024]{2,1,0:T(8,128)(2,1)S(1)} %copy-done), kind=kOutput, calls=%fused_computation.10 | convolution fusion | flops 2147483648 | bytes 8388608 | tf_op jit(solution)/shard_map/th,dh->td/dot_general | solution.py:84
  61.1 0.0 copy-done.7
  61.1 4.3 %fusion.17 = f32[1024,1024]{1,0:T(8,128)} fusion(f32[1024,1024]{1,0:T(8,128)S(1)} %fusion.7, bf16[1,1024,1024]{2,1,0:T(8,128)(2,1)S(1)} %copy-done.7, bf16[128,8,8,128]{3,2,1,0:T(8,128)(2,1)S(1)} %bitcast.61), kind=kOutput, calls=%fused_computation.22 | convolution fusion | flops 2148532224 | bytes 12582912 | tf_op jit(solution)/shard_map/th,dh->td/dot_general | solution.py:78
  65.4 0.0 reduce-scatter.2.cloned.1.call-update
  65.4 92.8 %reduce-scatter.2.cloned.1.call-done = f32[2,64,1024]{2,1,0:T(8,128)} async-done(((f32[2,512,1024]{2,1,0:T(8,128)}), f32[2,64,1024]{2,1,0:T(8,128)}) %reduce-scatter.2.cloned.1.call-update) | async-done | bytes 524304 | tf_op jit(solution)/shard_map/reduce_scatter | solution.py:91
  158.2 1.3 reshape.74
  159.5 1.3 copy.77
  160.8 1.9 reshape.78
  162.7 26.2 %all_to_all.11 = f32[16,1,8192]{2,1,0:T(1,128)S(1)} all-to-all(f32[16,1,8192]{2,1,0:T(1,128)S(1)} %reshape.78), channel_id=1, replica_groups=mesh['section'=8,'tensor'=16,'dp'=2] {'tensor'}, dimensions={0} | all-to-all | bytes 1048576 | tf_op jit(solution)/shard_map/all_to_all | solution.py:20
  188.9 0.0 copy-start.5
  188.9 0.0 copy-start.6
  188.9 0.5 broadcast.40
  189.5 2.8 %reduce.1 = f32[16,8192]{1,0:T(8,128)} reduce(f32[16,1,8192]{2,1,0:T(1,128)S(1)} %all_to_all.11, f32[]{:T(128)} %broadcast.40), dimensions={1}, to_apply=%all_to_all.7.reduce_sub_computation | reduce | bytes 1048580 | tf_op jit(solution)/shard_map/all_to_all | solution.py:20
  192.2 1.5 reshape.79
  193.7 0.1 reduce_sum.56
  193.8 0.0 copy-done.5
  193.8 0.0 copy-done.6
  193.8 0.1 multiply_reduce_fusion.1
  193.9 0.1 reshape.75
  194.0 0.1 reshape.76
  194.1 10.1 %all_to_all.12 = f32[16,1,256]{2,1,0:T(1,128)S(1)} all-to-all(f32[16,1,256]{2,1,0:T(1,128)S(1)} %broadcast_in_dim.2), channel_id=1, replica_groups=mesh['section'=8,'tensor'=16,'dp'=2] {'tensor'}, dimensions={0} | all-to-all | bytes 32768 | tf_op jit(solution)/shard_map/all_to_all | solution.py:26
  204.3 0.1 rsqrt.14
  204.3 0.1 reshape.77
  204.4 0.7 multiply_subtract_fusion
  (5 shorter events, 0.1 us)
Async XLA Ops:
  6.5 52.2 %copy-start = (bf16[1,1024,1024]{2,1,0:T(8,128)(2,1)S(1)}, bf16[1,1024,1024]{2,1,0:T(8,128)(2,1)}, u32[]{:S(2)}) copy-start(bf16[1,1024,1024]{2,1,0:T(8,128)(2,1)} %param.13) | copy-start | bytes 6291460
  6.5 151.7 %reduce-scatter.2.cloned.1.call-start = ((), (), s32[]{:S(2)}) async-start(), calls=%async_computation.3 | async-start | bytes 4718592 | tf_op jit(solution)/shard_map/reduce_scatter | solution.py:91
  6.5 3.7 %copy-start.3 = (bf16[1,2,512,1024]{3,2,1,0:T(8,128)(2,1)S(1)}, bf16[1,2,512,1024]{3,2,1,0:T(8,128)(2,1)}, u32[]{:S(2)}) copy-start(bf16[1,2,512,1024]{3,2,1,0:T(8,128)(2,1)} %param.9) | copy-start | bytes 6291460
  30.8 6.9 %copy-start.1 = (bf16[1,2,512,1024]{2,3,1,0:T(8,128)(2,1)S(1)}, bf16[1,2,512,1024]{2,3,1,0:T(8,128)(2,1)}, u32[]{:S(2)}) copy-start(bf16[1,2,512,1024]{2,3,1,0:T(8,128)(2,1)} %copy.65) | copy-start | bytes 6291460
  37.7 3.7 %copy-start.2 = (bf16[1,2,512,1024]{2,3,1,0:T(8,128)(2,1)S(1)}, bf16[1,2,512,1024]{2,3,1,0:T(8,128)(2,1)}, u32[]{:S(2)}) copy-start(bf16[1,2,512,1024]{2,3,1,0:T(8,128)(2,1)} %copy.88) | copy-start | bytes 6291460
  54.2 3.1 %copy-start.4 = (bf16[2,512,8,128]{3,1,2,0:T(8,128)(2,1)S(1)}, bf16[2,512,8,128]{3,1,2,0:T(8,128)(2,1)}, u32[]{:S(2)}) copy-start(bf16[2,512,8,128]{3,1,2,0:T(8,128)(2,1)} %convert_bitcast_fusion) | copy-start | bytes 6291460
  58.7 2.4 %copy-start.7 = (bf16[1,1024,1024]{2,1,0:T(8,128)(2,1)S(1)}, bf16[1,1024,1024]{2,1,0:T(8,128)(2,1)}, u32[]{:S(2)}) copy-start(bf16[1,1024,1024]{2,1,0:T(8,128)(2,1)} %param.12) | copy-start | bytes 6291460
  188.9 4.8 %copy-start.5 = (f32[2,64,64]{2,1,0:T(8,128)S(1)}, f32[2,64,64]{2,1,0:T(8,128)}, u32[]{:S(2)}) copy-start(f32[2,64,64]{2,1,0:T(8,128)} %param.14) | copy-start | bytes 98308
  188.9 4.8 %copy-start.6 = (f32[64]{0:T(128)S(1)}, f32[64]{0:T(128)}, u32[]{:S(2)}) copy-start(f32[64]{0:T(128)} %param.15) | copy-start | bytes 772
Sparse Core Ops, SparseCore 0:
  65.5 92.6 reduce-scatter.1
where the time goes:
time: 212 us
  waiting for transfers between devices  92.8 us (44%)
  blocking collectives  36.3 us (17%)
  matrix products  33.9 us (16%)
  local copies, waits for them, and re-layouts  24.9 us (12%)
  between operations  13.5 us (6%)
  other arithmetic  10.6 us (5%)
    reduce_scatter x1, waiting for transfers between devices, per_device(): lax.psum_scatter(partial_value, 'section', scatter_dimension=1, tiled=True)  92.8 us
    all_to_all x1, blocking collectives, sent_and_summed(): lax.all_to_all(in_blocks(shard, dim, peers), axis, 0, 0, tiled=True)  26.2 us
    unnamed x21, local copies, waits for them, and re-layouts  13 us
    dot_general x1, matrix products, per_device(): jnp.einsum('bhqk,bqhd->bkhd', score_low, query_heads, preferred_element_t...  11.6 us
    sub x1, matrix products, per_device(): shifted = jnp.exp(scores - jnp.max(scores, axis=-1, keepdims=True))  10.7 us
    all_to_all x1, blocking collectives, from_everyone(): return lax.all_to_all(copies, axis, split_axis=0, concat_axis=0, tiled=True)  10.1 us
    convert_element_type x1, other arithmetic, per_device(): probs_low = attn_probs.astype(jnp.bfloat16)  6.84 us
    dot_general x1, matrix products, per_device(): jnp.einsum('th,dh->td', key_grad.reshape(flat_rows, hidden_here), key_wei...  4.29 us
  transfers between devices with their start and end apart: 1, of which 1 were waited for; matrix products, arithmetic and copies ran while one was open for 0% of the time, Pallas kernels for 0%

commit v1 on v0

v1 whole, which is shorter than its diff:
```python
import functools

import jax
import jax.numpy as jnp
from jax import lax
from jax.experimental import pallas as pl
from jax.experimental.pallas import tpu as pltpu
from jax.sharding import PartitionSpec as P

D = 1024
DK = 128
EPS = 1e-06
F32 = jnp.float32
BF16 = jnp.bfloat16
MESH = pl.DeviceIdType.MESH

NSEQ = 2
HEADS = 8
ROWS = 512
NJ = 4
CW = D // NJ
NT = (((1,), (1,)), ((), ()))
NN = (((1,), (0,)), ((), ()))


def dot(a, b, dims, **kw):
    return lax.dot_general(a, b, dims, preferred_element_type=F32, **kw)


def kernel(
    q_hbm, k_hbm, v_hbm, g_hbm, wk_hbm, wv_hbm, hid_ref, gain_ref, out_ref,
    qs, ks, vs, gs, wks, wvs, kg, vg,
    part, d2dr, acc, r1, fin, xs, yr, zs, zr, cs, cr, hs, hg, gh, crossp, osend, orecv,
    in_sem, w_sem, d2d_s, d2d_r, x_s, x_r, y_s, y_r, z_s, z_r, c_s, c_r, h_s, h_r, o_s, o_r,
):
    section = lax.axis_index("section")
    tensor = lax.axis_index("tensor")
    yh, x = section // 4, section % 4
    z, c = tensor // 2, tensor % 2
    xp, xm, x2 = (x + 1) % 4, (x + 3) % 4, (x + 2) % 4
    to_core = {"tensor": z * 2 + (1 - c)}
    to_xp = {"section": yh * 4 + xp}
    to_xm = {"section": yh * 4 + xm}
    to_y = {"section": (1 - yh) * 4 + x}

    def loads(i):
        b, h = i // HEADS, i % HEADS
        cols = pl.ds(pl.multiple_of(h * DK, DK), DK)
        pairs = ((k_hbm, ks), (q_hbm, qs), (v_hbm, vs), (g_hbm, gs))
        return [
            pltpu.make_async_copy(src.at[0, b, :, cols], dst.at[i], in_sem.at[i, n])
            for n, (src, dst) in enumerate(pairs)
        ]

    def start_loads(i, _):
        for copy in loads(i):
            copy.start()
        return 0

    wcopies = [
        pltpu.make_async_copy(wk_hbm.at[0], wks, w_sem.at[0]),
        pltpu.make_async_copy(wv_hbm.at[0], wvs, w_sem.at[1]),
    ]
    lax.fori_loop(0, HEADS, start_loads, 0)
    for copy in wcopies:
        copy.start()
    lax.fori_loop(HEADS, NSEQ * HEADS, start_loads, 0)

    barrier = pltpu.get_barrier_semaphore()
    for peer in (to_xp, to_xm, to_y):
        pl.semaphore_signal(barrier, inc=1, device_id=peer, device_id_type=MESH)

    def greet(d, _):
        peer = {"tensor": (tensor + d) % 16}
        pl.semaphore_signal(barrier, inc=1, device_id=peer, device_id_type=MESH)
        return 0

    lax.fori_loop(1, 16, greet, 0)

    def send(src, dst, s, r, peer):
        return pltpu.make_async_remote_copy(
            src_ref=src, dst_ref=dst, send_sem=s, recv_sem=r, device_id=peer, device_id_type=MESH
        )

    def d2d_copy(b, j):
        return send(
            part.at[b, j, :, 1 - c], d2dr.at[b, j], d2d_s.at[b, j], d2d_r.at[b, j], to_core
        )

    def x_copy(b, j, n):
        a = acc.at[b, j]
        src, dst, peer = (
            (a.at[x2], r1.at[b, j, 0], to_xp),
            (a.at[4 + x2], r1.at[b, j, 1], to_xm),
            (a.at[4 + xp], fin.at[b, j, 0, 1], to_xp),
            (a.at[xm], fin.at[b, j, 1, 0], to_xm),
            (a.at[xp], fin.at[b, j, 0, 0], to_xp),
            (a.at[4 + xm], fin.at[b, j, 1, 1], to_xm),
        )[n]
        return send(src, dst, x_s.at[b, j, n], x_r.at[b, j, n], peer)

    def y_copy(b, j):
        return send(xs.at[b, j, 1 - yh], yr.at[b, j], y_s.at[b, j], y_r.at[b, j], to_y)

    def z_copy(b, zt):
        peer = {"tensor": zt * 2 + c}
        return send(zs.at[b, zt], zr.at[b, z], z_s.at[b, zt], z_r.at[b, z], peer)

    def z_recv(b, zt):
        peer = {"tensor": zt * 2 + c}
        return send(zs.at[b, zt], zr.at[b, zt], z_s.at[b, zt], z_r.at[b, zt], peer)

    def c_copy(zt):
        return send(cs, cr.at[z], c_s.at[zt], c_r.at[z], {"tensor": zt * 2 + c})

    def c_recv(zt):
        return send(cs, cr.at[zt], c_s.at[zt], c_r.at[zt], {"tensor": zt * 2 + c})

    def h_copy(t):
        return send(hs.at[t % 2], hg.at[tensor], h_s.at[t], h_r.at[tensor], {"tensor": t})

    def h_recv(t):
        return send(hs.at[t % 2], hg.at[t], h_s.at[t], h_r.at[t], {"tensor": t})

    def each(n, f):
        def body(i, _):
            f(i)
            return 0

        lax.fori_loop(0, n, body, 0)

    def project(b, j):
        at = pl.ds(pl.multiple_of(j * CW, CW), CW)
        p = dot(kg[...], wks[at, :], NT) + dot(vg[...], wvs[at, :], NT)
        part[b, j] = p.reshape(8, 2, 32, CW)
        d2d_copy(b, j).start()

    def stage1(b, j):
        d2d_copy(b, j).wait_recv()
        acc[b, j] = part[b, j, :, c] + d2dr[b, j]
        for n in range(4):
            x_copy(b, j, n).start()

    def stage2(b, j):
        x_copy(b, j, 0).wait_recv()
        acc[b, j, xp] = acc[b, j, xp] + r1[b, j, 0]
        x_copy(b, j, 4).start()
        x_copy(b, j, 1).wait_recv()
        acc[b, j, 4 + xm] = acc[b, j, 4 + xm] + r1[b, j, 1]
        x_copy(b, j, 5).start()

    def stage3(b, j):
        for n in range(2, 6):
            x_copy(b, j, n).wait_recv()
        for h in range(2):
            xs[b, j, h] = acc[b, j, h * 4 + x] + fin[b, j, 0, h] + fin[b, j, 1, h]
        y_copy(b, j).start()

    def stage4(b, j):
        y_copy(b, j).wait_recv()
        total = xs[b, j, yh] + yr[b, j]
        for n in range(CW // 128):
            zt = j * (CW // 128) + n
            block = total[:, n * 128 : (n + 1) * 128]
            zs[b, zt] = block
            crossp[pl.ds(b * 32, 32), :] += block * gh[b, zt]

            @pl.when(zt != z)
            def _():
                z_copy(b, zt).start()

    def head(i):
        for copy in loads(i):
            copy.wait()
        cols = pl.ds(pl.multiple_of((i % HEADS) * DK, DK), DK)
        scores = dot(ks[i], qs[i], NT)
        top = jnp.max(scores, axis=0, keepdims=True)
        shifted = jnp.exp(scores - top)
        probs = shifted * (1.0 / jnp.sum(shifted, axis=0, keepdims=True))
        probs_low = probs.astype(BF16)
        prob_grad = dot(vs[i], gs[i], NT)
        row_dot = jnp.sum(probs_low.astype(F32) * prob_grad, axis=0, keepdims=True)
        score_low = (probs * (prob_grad - row_dot)).astype(BF16)
        vg[:, cols] = dot(probs_low, gs[i], NN).astype(BF16)
        kg[:, cols] = dot(score_low, qs[i], NN).astype(BF16)

    def gather_hidden():
        gain8 = jnp.broadcast_to(gain_ref[...], (8, 64))
        for half in range(2):
            for b in range(NSEQ):
                hs[half, b * 32 : (b + 1) * 32] = hid_ref[b, half * 32 : (half + 1) * 32]
            hs[half, 64:72] = gain8

        def start(d):
            h_copy((tensor + d + 1) % 16).start()

        each(15, start)
        hg[tensor] = hs[c]

    def take_hidden():
        def wait(d):
            h_recv((tensor + d + 1) % 16).wait_recv()

        each(15, wait)
        for zt in range(8):
            both = jnp.concatenate([hg[2 * zt], hg[2 * zt + 1]], axis=-1)
            for b in range(NSEQ):
                gh[b, zt] = both[b * 32 : (b + 1) * 32] * both[64:65]
        crossp[...] = jnp.zeros_like(crossp)

    def step(i, _):
        @pl.when(i == HEADS)
        def _():
            pl.semaphore_wait(barrier, 18)
            gather_hidden()
            for copy in wcopies:
                copy.wait()
            each(NJ, lambda j: project(0, j))

        head(i)

        @pl.when(i == HEADS)
        def _():
            each(NJ, lambda j: stage1(0, j))

        @pl.when(i == HEADS + 3)
        def _():
            each(NJ, lambda j: stage2(0, j))

        @pl.when(i == HEADS + 6)
        def _():
            take_hidden()
            each(NJ, lambda j: stage3(0, j))

        return 0

    lax.fori_loop(0, NSEQ * HEADS, step, 0)

    for j in range(NJ):
        project(1, j)
        if j > 0:
            stage1(1, j - 1)
    stage1(1, NJ - 1)
    each(NJ, lambda j: stage4(0, j))
    for j in range(NJ):
        stage2(1, j)
    for j in range(NJ):
        stage3(1, j)
        if j > 0:
            stage4(1, j - 1)
    stage4(1, NJ - 1)

    cs[...] = dot(jnp.ones((8, 128), F32), crossp[...], NT, precision=lax.Precision.HIGHEST)

    def start_cross(d):
        c_copy((z + d + 1) % 8).start()

    each(7, start_cross)

    mine = jnp.concatenate([hg[2 * z], hg[2 * z + 1]], axis=-1)
    square = jnp.zeros((64, 64), F32)
    for t in range(16):
        part_of = hg[t, :64]
        square = square + part_of * part_of
    square = jnp.sum(square, axis=-1, keepdims=True)
    inverse = lax.rsqrt(square * (1.0 / D) + EPS)

    def wait_z(d):
        zt = (z + d + 1) % 8
        z_recv(0, zt).wait_recv()
        z_recv(1, zt).wait_recv()
        c_recv(zt).wait_recv()

    each(7, wait_z)
    zr[0, z] = zs[0, z]
    zr[1, z] = zs[1, z]
    cr[z] = cs[...]
    cross = cr[0]
    for t in range(1, 8):
        cross = cross + cr[t]
    wide = jnp.broadcast_to(cross[:1], (64, 128))
    row = lax.broadcasted_iota(jnp.int32, (64, 128), 0)
    lane = lax.broadcasted_iota(jnp.int32, (64, 128), 1)
    cross_col = jnp.sum(jnp.where(row == lane, wide, 0.0), axis=-1, keepdims=True)
    gain_mine, hid_mine = mine[64:65], mine[:64]
    scale = cross_col * inverse * inverse * inverse * (1.0 / D)
    for b in range(NSEQ):
        rows = slice(b * 32, (b + 1) * 32)
        grad = zr[b, 0]
        for t in range(1, 8):
            grad = grad + zr[b, t]
        done = gain_mine * grad * inverse[rows] - hid_mine[rows] * scale[rows]
        own = jnp.where(c == 0, done[:, :64], done[:, 64:])
        osend[b] = jnp.where(c == 0, done[:, 64:], done[:, :64])
        out_ref[b, pl.ds(pl.multiple_of(c * 32, 32), 32), :] = own
    o_copy = send(osend, orecv, o_s, o_r, to_core)
    o_copy.start()

    def sends(n):
        b, j = n // NJ, n % NJ
        d2d_copy(b, j).wait_send()
        y_copy(b, j).wait_send()
        for k in range(6):
            x_copy(b, j, k).wait_send()

    each(NSEQ * NJ, sends)

    def small_sends(d):
        zt = (z + d + 1) % 8
        z_copy(0, zt).wait_send()
        z_copy(1, zt).wait_send()
        c_copy(zt).wait_send()

    each(7, small_sends)
    each(15, lambda d: h_copy((tensor + d + 1) % 16).wait_send())
    o_copy.wait()
    for b in range(NSEQ):
        out_ref[b, pl.ds(pl.multiple_of((1 - c) * 32, 32), 32), :] = orecv[b]


def per_device(q, k, v, g, wk, wv, hidden, gain):
    dma = pltpu.SemaphoreType.DMA
    vm = pltpu.VMEM
    anywhere = pl.BlockSpec(memory_space=pl.ANY)
    vmem = pl.BlockSpec(memory_space=pltpu.VMEM)
    heads = vm((NSEQ * HEADS, ROWS, DK), BF16)
    return pl.pallas_call(
        kernel,
        out_shape=jax.ShapeDtypeStruct((NSEQ, 64, 64), F32),
        in_specs=[anywhere] * 6 + [vmem] * 2,
        out_specs=vmem,
        scratch_shapes=[
            heads, heads, heads, heads,
            vm((D, D), BF16), vm((D, D), BF16),
            vm((ROWS, D), BF16), vm((ROWS, D), BF16),
            vm((NSEQ, NJ, 8, 2, 32, CW), F32),
            vm((NSEQ, NJ, 8, 32, CW), F32),
            vm((NSEQ, NJ, 8, 32, CW), F32),
            vm((NSEQ, NJ, 2, 32, CW), F32),
            vm((NSEQ, NJ, 2, 2, 32, CW), F32),
            vm((NSEQ, NJ, 2, 32, CW), F32),
            vm((NSEQ, NJ, 32, CW), F32),
            vm((NSEQ, 8, 32, 128), F32),
            vm((NSEQ, 8, 32, 128), F32),
            vm((8, 128), F32),
            vm((8, 8, 128), F32),
            vm((2, 72, 64), F32),
            vm((16, 72, 64), F32),
            vm((NSEQ, 8, 32, 128), F32),
            vm((128, 128), F32),
            vm((NSEQ, 32, 64), F32),
            vm((NSEQ, 32, 64), F32),
            dma((NSEQ * HEADS, 4)), dma((2,)),
            dma((NSEQ, NJ)), dma((NSEQ, NJ)),
            dma((NSEQ, NJ, 6)), dma((NSEQ, NJ, 6)),
            dma((NSEQ, NJ)), dma((NSEQ, NJ)),
            dma((NSEQ, 8)), dma((NSEQ, 8)),
            dma((8,)), dma((8,)),
            dma((16,)), dma((16,)),
            dma, dma,
        ],
        compiler_params=pltpu.CompilerParams(
            collective_id=0, has_side_effects=True, vmem_limit_bytes=56 * 1024 * 1024
        ),
    )(q, k, v, g, wk, wv, hidden, gain.reshape(1, 64))


def solution(mesh):
    return jax.shard_map(
        per_device,
        mesh=mesh,
        in_specs=(
            P("section", "dp", None, "tensor"),
            P("section", "dp", None, "tensor"),
            P("section", "dp", None, "tensor"),
            P("section", "dp", None, "tensor"),
            P("section", None, "tensor"),
            P("section", None, "tensor"),
            P("dp", "section", "tensor"),
            P("tensor"),
        ),
        out_specs=P("dp", "section", "tensor"),
        check_vma=False,
    )
```

time: 212 us -> 67.3 us (0.32)
  waiting for transfers between devices: 92.8 us -> 0 us
  Pallas kernels: 0 us -> 65.6 us
  blocking collectives: 36.3 us -> 0 us
  matrix products: 33.9 us -> 0 us
  local copies, waits for them, and re-layouts: 24.9 us -> 1.47 us
  between operations: 13.5 us -> 0.01 us
  other arithmetic: 10.6 us -> 0 us
    reduce_scatter x1 -> x0, waiting for transfers between devices: 92.8 us -> none  [per_device(): lax.psum_scatter(partial_value, 'section', scatter_dimension=1, tiled=True)]
    pallas_call x0 -> x1, Pallas kernels: none -> 65.6 us  [per_device(): pl.pallas_call(kernel, out_shape=jax.ShapeDtypeStruct((NSEQ, 64, 64), F32...]
    all_to_all x2 -> x0, blocking collectives: 36.3 us -> none  [the longest x1 26.2 us: sent_and_summed(): lax.all_to_all(in_blocks(shard, dim, peers), axis, 0, 0, tiled=True)]
    dot_general x5 -> x0, matrix products: 23.2 us -> none  [the longest x1 11.6 us: per_device(): jnp.einsum('bhqk,bqhd->bkhd', score_low, query_heads, preferred_element_t...]
    unnamed x21 -> x1, local copies, waits for them, and re-layouts: 13 us -> 1.47 us
    sub x1 -> x0, matrix products: 10.7 us -> none  [per_device(): shifted = jnp.exp(scores - jnp.max(scores, axis=-1, keepdims=True))]
    convert_element_type x1 -> x0, other arithmetic: 6.84 us -> none  [per_device(): probs_low = attn_probs.astype(jnp.bfloat16)]
    convert_element_type x2 -> x0, local copies, waits for them, and re-layouts: 4.45 us -> none  [the longest x1 3.09 us: per_device(): key_grad = jnp.einsum('bhqk,bqhd->bkhd', score_low, query_heads, preferre...]
  transfers between devices with their start and end apart: 1 -> 0, of which waited for: 1 -> 0; matrix products, arithmetic and copies ran while one was open for 0% -> 0% of each run, Pallas kernels for 0% -> 0%
where the time goes in v1:
time: 67.3 us; the launch traced here: 67.1 us
  Pallas kernels  65.6 us (97%)
  local copies, waits for them, and re-layouts  1.47 us (2%)
    pallas_call x1, Pallas kernels, per_device(): pl.pallas_call(kernel, out_shape=jax.ShapeDtypeStruct((NSEQ, 64, 64), F32...  65.6 us
    unnamed x1, local copies, waits for them, and re-layouts  1.47 us

profile of v1, /device:TPU:1, one launch (start us, length us, event | category | flops | bytes accessed | tf_op | source)
XLA Modules:
  0.0 67.1 jit_solution(7355672991489963704)
XLA Ops:
  0.0 65.6 %shard_map.82 = f32[2,64,64]{2,1,0:T(8,128)} custom-call(bf16[1,2,512,1024]{3,2,1,0:T(8,128)(2,1)} %q_hbm.1, bf16[1,2,512,1024]{3,2,1,0:T(8,128)(2,1)} %k_hbm.1, bf16[1,2,512,1024]{3,2,1,0:T(8,128)(2,1)} %v_hbm.1, bf16[1,2,512,1024]{3,2,1,0:T(8,128)(2,1)} %g_hbm.1, bf16[1,1024,1024]{2,1,0:T(8,128)(2,1)} %wk_hbm.1, bf16[1,1024,1024]{2,1,0:T(8,128)(2,1)} %wv_hbm.1, ...), custom_call_target="tpu_custom_call" | custom-call | tf_op jit(solution)/shard_map/pallas_call | solution.py:327
  65.6 1.5 %copy.10 = f32[2,64,64]{2,1,0:T(8,128)} copy(f32[2,64,64]{2,1,0:T(8,128)} %shard_map.82) | data formatting | bytes 65536

commit v2 on v1

v2 whole, which is shorter than its diff:
```python
import functools

import jax
import jax.numpy as jnp
from jax import lax
from jax.experimental import pallas as pl
from jax.experimental.pallas import tpu as pltpu
from jax.sharding import PartitionSpec as P

D = 1024
DK = 128
EPS = 1e-06
F32 = jnp.float32
BF16 = jnp.bfloat16
MESH = pl.DeviceIdType.MESH

NSEQ = 2
HEADS = 8
ROWS = 512
NJ = 4
CW = D // NJ
NT = (((1,), (1,)), ((), ()))
NN = (((1,), (0,)), ((), ()))


def dot(a, b, dims, **kw):
    return lax.dot_general(a, b, dims, preferred_element_type=F32, **kw)


def kernel(
    q_hbm, k_hbm, v_hbm, g_hbm, wk_hbm, wv_hbm, hid_ref, gain_ref, out_hbm,
    kqvg, wks, wvs, kg, vg,
    part, d2dr, acc, r1, fin, zs, zr, cs, cr, hs, hp, hg, gh, crossp, oown, osend,
    in_sem, w_sem, d2d_s, d2d_r, x_s, r1_r, fin_r, z_s, z_r, c_s, c_r,
    p_s, p_r, hy_s, hy_r, h_s, h_r, o_l, o_s, o_r,
):
    section = lax.axis_index("section")
    tensor = lax.axis_index("tensor")
    yh, x = section // 4, section % 4
    z, c = tensor // 2, tensor % 2
    xp, xm, x2 = (x + 1) % 4, (x + 3) % 4, (x + 2) % 4
    me = yh * 8 + z
    to_core = {"tensor": z * 2 + (1 - c)}
    to_xp = {"section": yh * 4 + xp}
    to_xm = {"section": yh * 4 + xm}
    to_y = {"section": (1 - yh) * 4 + x}

    def to_yz(n):
        return {"section": n // 8 * 4 + x, "tensor": n % 8 * 2 + c}

    def each(n, f, start=0):
        def body(i, _):
            f(i)
            return 0

        lax.fori_loop(start, n, body, 0)

    def wait_bytes(ref, sem):
        pltpu.make_async_copy(ref, ref, sem).wait()

    def load(i):
        b, h = i // HEADS, i % HEADS
        cols = pl.ds(pl.multiple_of(h * DK, DK), DK)
        for n, src in enumerate((k_hbm, q_hbm, v_hbm, g_hbm)):
            pltpu.make_async_copy(src.at[0, b, :, cols], kqvg.at[i, n], in_sem.at[i]).start()

    wcopies = [
        pltpu.make_async_copy(wk_hbm.at[0], wks, w_sem.at[0]),
        pltpu.make_async_copy(wv_hbm.at[0], wvs, w_sem.at[1]),
    ]
    each(HEADS, load)
    for copy in wcopies:
        copy.start()
    each(NSEQ * HEADS, load, HEADS)

    barrier = pltpu.get_barrier_semaphore()
    for peer in (to_core, to_xp, to_xm):
        pl.semaphore_signal(barrier, inc=1, device_id=peer, device_id_type=MESH)

    def greet(d):
        peer = to_yz((me + d) % 16)
        pl.semaphore_signal(barrier, inc=1, device_id=peer, device_id_type=MESH)

    each(16, greet, 1)

    def send(src, dst, s, r, peer):
        return pltpu.make_async_remote_copy(
            src_ref=src, dst_ref=dst, send_sem=s, recv_sem=r, device_id=peer, device_id_type=MESH
        )

    def x_copy(b, j, n):
        a = acc.at[b, j]
        src, dst, r, peer = (
            (a.at[x2], r1.at[b, j, 0], r1_r.at[b, j, 0], to_xp),
            (a.at[4 + x2], r1.at[b, j, 1], r1_r.at[b, j, 1], to_xm),
            (a.at[4 + xp], fin.at[b, j, 0, 1], fin_r.at[b, j], to_xp),
            (a.at[xm], fin.at[b, j, 1, 0], fin_r.at[b, j], to_xm),
            (a.at[xp], fin.at[b, j, 0, 0], fin_r.at[b, j], to_xp),
            (a.at[4 + xm], fin.at[b, j, 1, 1], fin_r.at[b, j], to_xm),
        )[n]
        return send(src, dst, x_s, r, peer)

    def project(b, j):
        at = pl.ds(pl.multiple_of(j * CW, CW), CW)
        p = dot(kg[...], wks[at, :], NT) + dot(vg[...], wvs[at, :], NT)
        part[b, j] = p.reshape(8, 2, 32, CW)
        send(part.at[b, j, :, 1 - c], d2dr.at[b, j], d2d_s, d2d_r.at[b, j], to_core).start()

    def stage1(b, j):
        wait_bytes(d2dr.at[b, j], d2d_r.at[b, j])
        acc[b, j] = part[b, j, :, c] + d2dr[b, j]
        for n in range(2):
            x_copy(b, j, n).start()

    def stage1b(b, j):
        for n in range(2, 4):
            x_copy(b, j, n).start()

    def stage2(b, j):
        wait_bytes(r1.at[b, j, 0], r1_r.at[b, j, 0])
        acc[b, j, xp] = acc[b, j, xp] + r1[b, j, 0]
        x_copy(b, j, 4).start()
        wait_bytes(r1.at[b, j, 1], r1_r.at[b, j, 1])
        acc[b, j, 4 + xm] = acc[b, j, 4 + xm] + r1[b, j, 1]
        x_copy(b, j, 5).start()

    def stage3(b, j):
        wait_bytes(fin.at[b, j], fin_r.at[b, j])
        for k in range(2):
            h = (1 - yh) if k == 0 else yh
            total = acc[b, j, h * 4 + x] + fin[b, j, 0, h] + fin[b, j, 1, h]
            for n in range(CW // 128):
                zt = j * (CW // 128) + n
                to = h * 8 + zt
                block = total[:, n * 128 : (n + 1) * 128]
                zs[b, to] = block
                crossp[h, pl.ds(pl.multiple_of(b * 32, 32), 32), :] += block * gh[b, h, zt]

                @pl.when(to != me)
                def _():
                    send(zs.at[b, to], zr.at[b, me], z_s, z_r, to_yz(to)).start()

    def head(i):
        wait_bytes(kqvg.at[i], in_sem.at[i])
        cols = pl.ds(pl.multiple_of((i % HEADS) * DK, DK), DK)
        scores = dot(kqvg[i, 0], kqvg[i, 1], NT)
        top = jnp.max(scores, axis=0, keepdims=True)
        shifted = jnp.exp(scores - top)
        probs = shifted * (1.0 / jnp.sum(shifted, axis=0, keepdims=True))
        probs_low = probs.astype(BF16)
        prob_grad = dot(kqvg[i, 2], kqvg[i, 3], NT)
        row_dot = jnp.sum(probs_low.astype(F32) * prob_grad, axis=0, keepdims=True)
        score_low = (probs * (prob_grad - row_dot)).astype(BF16)
        vg[:, cols] = dot(probs_low, kqvg[i, 3], NN).astype(BF16)
        kg[:, cols] = dot(score_low, kqvg[i, 1], NN).astype(BF16)

    def swap_hidden():
        gain8 = jnp.broadcast_to(gain_ref[...], (8, 64))
        for half in range(2):
            for b in range(NSEQ):
                hs[half, b * 32 : (b + 1) * 32] = hid_ref[b, half * 32 : (half + 1) * 32]
            hs[half, 64:72] = gain8
        send(hs.at[1 - c], hp, p_s, p_r, to_core).start()

    def y_rows():
        return hg.at[z, pl.ds(pl.multiple_of(yh * 64, 64), 64)]

    def swap_hidden_y():
        wait_bytes(hp, p_r)
        own, other = hs[c], hp[...]
        both = jnp.where(
            c == 0,
            jnp.concatenate([own, other], axis=-1),
            jnp.concatenate([other, own], axis=-1),
        )
        hg[z, pl.ds(pl.multiple_of(yh * 64, 64), 64), :] = both[:64]
        hg[z, 128:136] = both[64:]
        send(y_rows(), y_rows(), hy_s, hy_r, to_y).start()

    def gather_hidden():
        wait_bytes(y_rows(), hy_r)

        def start(d):
            zt = (z + d) % 8
            send(hg.at[z], hg.at[z], h_s, h_r, {"tensor": zt * 2 + c}).start()

        each(8, start, 1)

    def take_hidden():
        wait_bytes(hg.at[pl.ds(0, 7)], h_r)
        for zt in range(8):
            for h in range(2):
                for b in range(NSEQ):
                    at = h * 64 + b * 32
                    gh[b, h, zt] = hg[zt, at : at + 32] * hg[zt, 128:129]
        crossp[...] = jnp.zeros_like(crossp)

    def step(i, _):
        @pl.when(i == 3)
        def _():
            pl.semaphore_wait(barrier, 18)
            swap_hidden()

        @pl.when(i == 5)
        def _():
            swap_hidden_y()

        @pl.when(i == 7)
        def _():
            gather_hidden()

        @pl.when(i == HEADS)
        def _():
            for copy in wcopies:
                copy.wait()
            each(NJ, lambda j: project(0, j))

        head(i)

        @pl.when(i == HEADS)
        def _():
            each(NJ, lambda j: stage1(0, j))
            each(NJ, lambda j: stage1b(0, j))

        @pl.when(i == HEADS + 4)
        def _():
            each(NJ, lambda j: stage2(0, j))

        @pl.when(i == HEADS + 7)
        def _():
            take_hidden()
            each(NJ, lambda j: stage3(0, j))

        return 0

    lax.fori_loop(0, NSEQ * HEADS, step, 0)

    def tail(t):
        @pl.when(t < NJ)
        def _():
            project(1, t)

        @pl.when((t >= 2) & (t < NJ + 2))
        def _():
            stage1(1, t - 2)
            stage1b(1, t - 2)

        @pl.when((t >= 3) & (t < NJ + 3))
        def _():
            stage2(1, t - 3)

        @pl.when(t >= 5)
        def _():
            stage3(1, t - 5)

    each(NJ + 5, tail)

    for h in range(2):
        cs[h] = dot(jnp.ones((8, 128), F32), crossp[h], NT, precision=lax.Precision.HIGHEST)

    def start_cross(d):
        to = (me + d) % 16
        send(cs.at[to // 8], cr.at[me], c_s, c_r, to_yz(to)).start()

    each(16, start_cross, 1)

    rows = pl.ds(pl.multiple_of(yh * 64, 64), 64)
    hid_mine, gain_mine = hg[z, rows, :], hg[z, 128:129]
    square = jnp.zeros((64, 128), F32)
    for zt in range(8):
        hidden = hg[zt, rows, :]
        square = square + hidden * hidden
    square = jnp.sum(square, axis=-1, keepdims=True)
    inverse = lax.rsqrt(square * (1.0 / D) + EPS)

    def finish():
        wait_bytes(zr.at[:, pl.ds(0, 15)], z_r)
        wait_bytes(cr.at[pl.ds(0, 15)], c_r)

    finish()
    for b in range(NSEQ):
        zr[b, me] = zs[b, me]
    cr[me] = cs[yh]
    cross = cr[0]
    for t in range(1, 16):
        cross = cross + cr[t]
    wide = jnp.broadcast_to(cross[:1], (64, 128))
    row = lax.broadcasted_iota(jnp.int32, (64, 128), 0)
    lane = lax.broadcasted_iota(jnp.int32, (64, 128), 1)
    cross_col = jnp.sum(jnp.where(row == lane, wide, 0.0), axis=-1, keepdims=True)
    scale = cross_col * inverse * inverse * inverse * (1.0 / D)
    for b in range(NSEQ):
        at = slice(b * 32, (b + 1) * 32)
        grad = zr[b, 0]
        for t in range(1, 16):
            grad = grad + zr[b, t]
        done = gain_mine * grad * inverse[at] - hid_mine[at] * scale[at]
        oown[b] = jnp.where(c == 0, done[:, :64], done[:, 64:])
        osend[b] = jnp.where(c == 0, done[:, 64:], done[:, :64])
    half = out_hbm.at[:, pl.ds(pl.multiple_of(c * 32, 32), 32), :]
    other = out_hbm.at[:, pl.ds(pl.multiple_of((1 - c) * 32, 32), 32), :]
    away = send(osend, half, o_s, o_r, to_core)
    away.start()
    here = pltpu.make_async_copy(oown, half, o_l)
    here.start()

    wait_bytes(d2dr, d2d_s)
    wait_bytes(acc.at[:, :, pl.ds(0, 6)], x_s)
    wait_bytes(zs.at[:, pl.ds(0, 15)], z_s)
    wait_bytes(cr.at[pl.ds(0, 15)], c_s)
    wait_bytes(hp, p_s)
    wait_bytes(y_rows(), hy_s)
    wait_bytes(hg.at[pl.ds(0, 7)], h_s)
    here.wait()
    away.wait_send()
    wait_bytes(other, o_r)


def per_device(q, k, v, g, wk, wv, hidden, gain):
    dma = pltpu.SemaphoreType.DMA
    vm = pltpu.VMEM
    anywhere = pl.BlockSpec(memory_space=pl.ANY)
    vmem = pl.BlockSpec(memory_space=pltpu.VMEM)
    return pl.pallas_call(
        kernel,
        out_shape=jax.ShapeDtypeStruct((NSEQ, 64, 64), F32),
        in_specs=[anywhere] * 6 + [vmem] * 2,
        out_specs=anywhere,
        scratch_shapes=[
            vm((NSEQ * HEADS, 4, ROWS, DK), BF16),
            vm((D, D), BF16), vm((D, D), BF16),
            vm((ROWS, D), BF16), vm((ROWS, D), BF16),
            vm((NSEQ, NJ, 8, 2, 32, CW), F32),
            vm((NSEQ, NJ, 8, 32, CW), F32),
            vm((NSEQ, NJ, 8, 32, CW), F32),
            vm((NSEQ, NJ, 2, 32, CW), F32),
            vm((NSEQ, NJ, 2, 2, 32, CW), F32),
            vm((NSEQ, 16, 32, 128), F32),
            vm((NSEQ, 16, 32, 128), F32),
            vm((2, 8, 128), F32),
            vm((16, 8, 128), F32),
            vm((2, 72, 64), F32),
            vm((72, 64), F32),
            vm((8, 136, 128), F32),
            vm((NSEQ, 2, 8, 32, 128), F32),
            vm((2, 128, 128), F32),
            vm((NSEQ, 32, 64), F32),
            vm((NSEQ, 32, 64), F32),
            dma((NSEQ * HEADS,)), dma((2,)),
            dma, dma((NSEQ, NJ)),
            dma, dma((NSEQ, NJ, 2)), dma((NSEQ, NJ)),
            dma, dma,
            dma, dma,
            dma, dma, dma, dma, dma, dma,
            dma, dma, dma,
        ],
        compiler_params=pltpu.CompilerParams(
            collective_id=0, has_side_effects=True, vmem_limit_bytes=56 * 1024 * 1024
        ),
    )(q, k, v, g, wk, wv, hidden, gain.reshape(1, 64))


def solution(mesh):
    return jax.shard_map(
        per_device,
        mesh=mesh,
        in_specs=(
            P("section", "dp", None, "tensor"),
            P("section", "dp", None, "tensor"),
            P("section", "dp", None, "tensor"),
            P("section", "dp", None, "tensor"),
            P("section", None, "tensor"),
            P("section", None, "tensor"),
            P("dp", "section", "tensor"),
            P("tensor"),
        ),
        out_specs=P("dp", "section", "tensor"),
        check_vma=False,
    )
```

time: 67.3 us -> 60.7 us (0.902)
  Pallas kernels: 65.6 us -> 59.1 us
    pallas_call x1, Pallas kernels: 65.6 us -> 59.1 us  [per_device(): pl.pallas_call(kernel, out_shape=jax.ShapeDtypeStruct((NSEQ, 64, 64), F32...]
where the time goes in v2:
time: 60.7 us; the launch traced here: 60.5 us
  Pallas kernels  59.1 us (97%)
  local copies, waits for them, and re-layouts  1.47 us (2%)
    pallas_call x1, Pallas kernels, per_device(): pl.pallas_call(kernel, out_shape=jax.ShapeDtypeStruct((NSEQ, 64, 64), F32...  59.1 us
    unnamed x1, local copies, waits for them, and re-layouts  1.47 us

profile of v2, /device:TPU:1, one launch (start us, length us, event | category | flops | bytes accessed | tf_op | source)
XLA Modules:
  0.0 60.5 jit_solution(8620490148240074686)
XLA Ops:
  0.0 59.1 %shard_map.82 = f32[2,64,64]{2,1,0:T(8,128)} custom-call(bf16[1,2,512,1024]{3,2,1,0:T(8,128)(2,1)} %q_hbm.1, bf16[1,2,512,1024]{3,2,1,0:T(8,128)(2,1)} %k_hbm.1, bf16[1,2,512,1024]{3,2,1,0:T(8,128)(2,1)} %v_hbm.1, bf16[1,2,512,1024]{3,2,1,0:T(8,128)(2,1)} %g_hbm.1, bf16[1,1024,1024]{2,1,0:T(8,128)(2,1)} %wk_hbm.1, bf16[1,1024,1024]{2,1,0:T(8,128)(2,1)} %wv_hbm.1, ...), custom_call_target="tpu_custom_call" | custom-call | tf_op jit(solution)/shard_map/pallas_call | solution.py:324
  59.1 1.5 %copy.10 = f32[2,64,64]{2,1,0:T(8,128)} copy(f32[2,64,64]{2,1,0:T(8,128)} %shard_map.82) | data formatting | bytes 65536

commit v3 on v2

--- a/solution.py
+++ b/solution.py
@@ -17,6 +17,7 @@
 NSEQ = 2
 HEADS = 8
 ROWS = 512
+GROUP = 4
 NJ = 4
 CW = D // NJ
 NT = (((1,), (1,)), ((), ()))
@@ -30,9 +31,9 @@
 def kernel(
     q_hbm, k_hbm, v_hbm, g_hbm, wk_hbm, wv_hbm, hid_ref, gain_ref, out_hbm,
     kqvg, wks, wvs, kg, vg,
-    part, d2dr, acc, r1, fin, zs, zr, cs, cr, hs, hp, hg, gh, crossp, oown, osend,
+    part, d2dr, acc, r1, fin, zs, zr, cs, cr, hs, hr, hg, gh, crossp, oown, osend,
     in_sem, w_sem, d2d_s, d2d_r, x_s, r1_r, fin_r, z_s, z_r, c_s, c_r,
-    p_s, p_r, hy_s, hy_r, h_s, h_r, o_l, o_s, o_r,
+    h_s, h_r, o_l, o_s, o_r,
 ):
     section = lax.axis_index("section")
     tensor = lax.axis_index("tensor")
@@ -40,6 +41,7 @@
     z, c = tensor // 2, tensor % 2
     xp, xm, x2 = (x + 1) % 4, (x + 3) % 4, (x + 2) % 4
     me = yh * 8 + z
+    me32 = yh * 16 + tensor
     to_core = {"tensor": z * 2 + (1 - c)}
     to_xp = {"section": yh * 4 + xp}
     to_xm = {"section": yh * 4 + xm}
@@ -69,19 +71,19 @@
         pltpu.make_async_copy(wv_hbm.at[0], wvs, w_sem.at[1]),
     ]
     each(HEADS, load)
+
+    barrier = pltpu.get_barrier_semaphore()
+    for peer in (to_xp, to_xm):
+        pl.semaphore_signal(barrier, inc=1, device_id=peer, device_id_type=MESH)
+
+    def greet(d):
+        to = (me32 + d) % 32
+        peer = {"section": to // 16 * 4 + x, "tensor": to % 16}
+        pl.semaphore_signal(barrier, inc=1, device_id=peer, device_id_type=MESH)
+
+    each(32, greet, 1)
     for copy in wcopies:
         copy.start()
-    each(NSEQ * HEADS, load, HEADS)
-
-    barrier = pltpu.get_barrier_semaphore()
-    for peer in (to_core, to_xp, to_xm):
-        pl.semaphore_signal(barrier, inc=1, device_id=peer, device_id_type=MESH)
-
-    def greet(d):
-        peer = to_yz((me + d) % 16)
-        pl.semaphore_signal(barrier, inc=1, device_id=peer, device_id_type=MESH)
-
-    each(16, greet, 1)
 
     def send(src, dst, s, r, peer):
         return pltpu.make_async_remote_copy(
@@ -141,7 +143,6 @@
                     send(zs.at[b, to], zr.at[b, me], z_s, z_r, to_yz(to)).start()
 
     def head(i):
-        wait_bytes(kqvg.at[i], in_sem.at[i])
         cols = pl.ds(pl.multiple_of((i % HEADS) * DK, DK), DK)
         scores = dot(kqvg[i, 0], kqvg[i, 1], NT)
         top = jnp.max(scores, axis=0, keepdims=True)
@@ -154,91 +155,80 @@
         vg[:, cols] = dot(probs_low, kqvg[i, 3], NN).astype(BF16)
         kg[:, cols] = dot(score_low, kqvg[i, 1], NN).astype(BF16)
 
-    def swap_hidden():
+    def gather_hidden():
         gain8 = jnp.broadcast_to(gain_ref[...], (8, 64))
         for half in range(2):
-            for b in range(NSEQ):
-                hs[half, b * 32 : (b + 1) * 32] = hid_ref[b, half * 32 : (half + 1) * 32]
-            hs[half, 64:72] = gain8
-        send(hs.at[1 - c], hp, p_s, p_r, to_core).start()
-
-    def y_rows():
-        return hg.at[z, pl.ds(pl.multiple_of(yh * 64, 64), 64)]
-
-    def swap_hidden_y():
-        wait_bytes(hp, p_r)
-        own, other = hs[c], hp[...]
-        both = jnp.where(
-            c == 0,
-            jnp.concatenate([own, other], axis=-1),
-            jnp.concatenate([other, own], axis=-1),
-        )
-        hg[z, pl.ds(pl.multiple_of(yh * 64, 64), 64), :] = both[:64]
-        hg[z, 128:136] = both[64:]
-        send(y_rows(), y_rows(), hy_s, hy_r, to_y).start()
-
-    def gather_hidden():
-        wait_bytes(y_rows(), hy_r)
+            at = slice(half * 32, (half + 1) * 32)
+            hs[half, :32] = jnp.concatenate([hid_ref[0, at], hid_ref[1, at]], axis=-1)
+            hs[half, 32:] = jnp.concatenate([gain8, gain8], axis=-1)
+        hr[me32] = hs[c]
 
         def start(d):
-            zt = (z + d) % 8
-            send(hg.at[z], hg.at[z], h_s, h_r, {"tensor": zt * 2 + c}).start()
-
-        each(8, start, 1)
+            to = (me32 + d) % 32
+            peer = {"section": to // 16 * 4 + x, "tensor": to % 16}
+            send(hs.at[to % 2], hr.at[me32], h_s, h_r, peer).start()
+
+        each(32, start, 1)
 
     def take_hidden():
-        wait_bytes(hg.at[pl.ds(0, 7)], h_r)
-        for zt in range(8):
-            for h in range(2):
-                for b in range(NSEQ):
-                    at = h * 64 + b * 32
-                    gh[b, h, zt] = hg[zt, at : at + 32] * hg[zt, 128:129]
+        wait_bytes(hr.at[pl.ds(0, 31)], h_r)
+        low = lax.broadcasted_iota(jnp.int32, (40, 128), 1) < 64
+        for h in range(2):
+            for zt in range(8):
+                even, odd = hr[h * 16 + 2 * zt], hr[h * 16 + 2 * zt + 1]
+                first = jnp.where(low, even, pltpu.roll(odd, 64, 1))
+                second = jnp.where(low, pltpu.roll(even, 64, 1), odd)
+                gain_row = first[32:33]
+                for b, hidden in enumerate((first[:32], second[:32])):
+                    hg[h, zt, b * 32 : (b + 1) * 32] = hidden
+                    gh[b, h, zt] = hidden * gain_row
+                hg[h, zt, 64:72] = first[32:]
         crossp[...] = jnp.zeros_like(crossp)
 
-    def step(i, _):
-        @pl.when(i == 3)
-        def _():
-            pl.semaphore_wait(barrier, 18)
-            swap_hidden()
-
-        @pl.when(i == 5)
-        def _():
-            swap_hidden_y()
-
-        @pl.when(i == 7)
-        def _():
+    def group(n):
+        @pl.when(n == 1)
+        def _():
+            pl.semaphore_wait(barrier, 33)
             gather_hidden()
 
-        @pl.when(i == HEADS)
+        @pl.when(n == HEADS // GROUP)
         def _():
             for copy in wcopies:
                 copy.wait()
-            each(NJ, lambda j: project(0, j))
-
-        head(i)
-
-        @pl.when(i == HEADS)
-        def _():
-            each(NJ, lambda j: stage1(0, j))
+
+            def first(t):
+                @pl.when(t < NJ)
+                def _():
+                    project(0, t)
+
+                @pl.when(t >= 2)
+                def _():
+                    stage1(0, t - 2)
+
+            each(NJ + 2, first)
             each(NJ, lambda j: stage1b(0, j))
 
-        @pl.when(i == HEADS + 4)
+        @pl.when(n == HEADS // GROUP + 1)
         def _():
             each(NJ, lambda j: stage2(0, j))
 
-        @pl.when(i == HEADS + 7)
-        def _():
-            take_hidden()
-            each(NJ, lambda j: stage3(0, j))
-
-        return 0
-
-    lax.fori_loop(0, NSEQ * HEADS, step, 0)
+        @pl.when(n < HEADS // GROUP)
+        def _():
+            each((n + 1) * GROUP + HEADS, load, n * GROUP + HEADS)
+
+        for k in range(GROUP):
+            wait_bytes(kqvg.at[n * GROUP + k], in_sem.at[n * GROUP + k])
+        for k in range(GROUP):
+            head(n * GROUP + k)
+
+    each(NSEQ * HEADS // GROUP, group)
+    take_hidden()
 
     def tail(t):
         @pl.when(t < NJ)
         def _():
             project(1, t)
+            stage3(0, t)
 
         @pl.when((t >= 2) & (t < NJ + 2))
         def _():
@@ -264,11 +254,10 @@
 
     each(16, start_cross, 1)
 
-    rows = pl.ds(pl.multiple_of(yh * 64, 64), 64)
-    hid_mine, gain_mine = hg[z, rows, :], hg[z, 128:129]
+    hid_mine, gain_mine = hg[yh, z, :64], hg[yh, z, 64:65]
     square = jnp.zeros((64, 128), F32)
     for zt in range(8):
-        hidden = hg[zt, rows, :]
+        hidden = hg[yh, zt, :64]
         square = square + hidden * hidden
     square = jnp.sum(square, axis=-1, keepdims=True)
     inverse = lax.rsqrt(square * (1.0 / D) + EPS)
@@ -308,9 +297,7 @@
     wait_bytes(acc.at[:, :, pl.ds(0, 6)], x_s)
     wait_bytes(zs.at[:, pl.ds(0, 15)], z_s)
     wait_bytes(cr.at[pl.ds(0, 15)], c_s)
-    wait_bytes(hp, p_s)
-    wait_bytes(y_rows(), hy_s)
-    wait_bytes(hg.at[pl.ds(0, 7)], h_s)
+    wait_bytes(hr.at[pl.ds(0, 31)], h_s)
     here.wait()
     away.wait_send()
     wait_bytes(other, o_r)
@@ -339,9 +326,9 @@
             vm((NSEQ, 16, 32, 128), F32),
             vm((2, 8, 128), F32),
             vm((16, 8, 128), F32),
-            vm((2, 72, 64), F32),
-            vm((72, 64), F32),
-            vm((8, 136, 128), F32),
+            vm((2, 40, 128), F32),
+            vm((32, 40, 128), F32),
+            vm((2, 8, 72, 128), F32),
             vm((NSEQ, 2, 8, 32, 128), F32),
             vm((2, 128, 128), F32),
             vm((NSEQ, 32, 64), F32),
@@ -351,7 +338,7 @@
             dma, dma((NSEQ, NJ, 2)), dma((NSEQ, NJ)),
             dma, dma,
             dma, dma,
-            dma, dma, dma, dma, dma, dma,
+            dma, dma,
             dma, dma, dma,
         ],
         compiler_params=pltpu.CompilerParams(

time: 60.7 us -> 57.2 us (0.942)
  Pallas kernels: 59.1 us -> 55.6 us
    pallas_call x1, Pallas kernels: 59.1 us -> 55.6 us  [per_device(): pl.pallas_call(kernel, out_shape=jax.ShapeDtypeStruct((NSEQ, 64, 64), F32...]
where the time goes in v3:
time: 57.2 us; the launch traced here: 57.1 us
  Pallas kernels  55.6 us (97%)
  local copies, waits for them, and re-layouts  1.47 us (3%)
    pallas_call x1, Pallas kernels, per_device(): pl.pallas_call(kernel, out_shape=jax.ShapeDtypeStruct((NSEQ, 64, 64), F32...  55.6 us
    unnamed x1, local copies, waits for them, and re-layouts  1.47 us

profile of v3, /device:TPU:1, one launch (start us, length us, event | category | flops | bytes accessed | tf_op | source)
XLA Modules:
  0.0 57.1 jit_solution(6235529267778950692)
XLA Ops:
  0.0 55.6 %shard_map.82 = f32[2,64,64]{2,1,0:T(8,128)} custom-call(bf16[1,2,512,1024]{3,2,1,0:T(8,128)(2,1)} %q_hbm.1, bf16[1,2,512,1024]{3,2,1,0:T(8,128)(2,1)} %k_hbm.1, bf16[1,2,512,1024]{3,2,1,0:T(8,128)(2,1)} %v_hbm.1, bf16[1,2,512,1024]{3,2,1,0:T(8,128)(2,1)} %g_hbm.1, bf16[1,1024,1024]{2,1,0:T(8,128)(2,1)} %wk_hbm.1, bf16[1,1024,1024]{2,1,0:T(8,128)(2,1)} %wv_hbm.1, ...), custom_call_target="tpu_custom_call" | custom-call | tf_op jit(solution)/shard_map/pallas_call | solution.py:311
  55.6 1.5 %copy.10 = f32[2,64,64]{2,1,0:T(8,128)} copy(f32[2,64,64]{2,1,0:T(8,128)} %shard_map.82) | data formatting | bytes 65536

commit v4 on v3

--- a/solution.py
+++ b/solution.py
@@ -37,9 +37,9 @@
 ):
     section = lax.axis_index("section")
     tensor = lax.axis_index("tensor")
-    yh, x = section // 4, section % 4
-    z, c = tensor // 2, tensor % 2
-    xp, xm, x2 = (x + 1) % 4, (x + 3) % 4, (x + 2) % 4
+    yh, x = lax.div(section, 4), lax.rem(section, 4)
+    z, c = lax.div(tensor, 2), lax.rem(tensor, 2)
+    xp, xm, x2 = lax.rem(x + 1, 4), lax.rem(x + 3, 4), lax.rem(x + 2, 4)
     me = yh * 8 + z
     me32 = yh * 16 + tensor
     to_core = {"tensor": z * 2 + (1 - c)}
@@ -48,7 +48,7 @@
     to_y = {"section": (1 - yh) * 4 + x}
 
     def to_yz(n):
-        return {"section": n // 8 * 4 + x, "tensor": n % 8 * 2 + c}
+        return {"section": lax.div(n, 8) * 4 + x, "tensor": lax.rem(n, 8) * 2 + c}
 
     def each(n, f, start=0):
         def body(i, _):
@@ -77,8 +77,8 @@
         pl.semaphore_signal(barrier, inc=1, device_id=peer, device_id_type=MESH)
 
     def greet(d):
-        to = (me32 + d) % 32
-        peer = {"section": to // 16 * 4 + x, "tensor": to % 16}
+        to = lax.rem(me32 + d, 32)
+        peer = {"section": lax.div(to, 16) * 4 + x, "tensor": lax.rem(to, 16)}
         pl.semaphore_signal(barrier, inc=1, device_id=peer, device_id_type=MESH)
 
     each(32, greet, 1)
@@ -164,9 +164,9 @@
         hr[me32] = hs[c]
 
         def start(d):
-            to = (me32 + d) % 32
-            peer = {"section": to // 16 * 4 + x, "tensor": to % 16}
-            send(hs.at[to % 2], hr.at[me32], h_s, h_r, peer).start()
+            to = lax.rem(me32 + d, 32)
+            peer = {"section": lax.div(to, 16) * 4 + x, "tensor": lax.rem(to, 16)}
+            send(hs.at[lax.rem(to, 2)], hr.at[me32], h_s, h_r, peer).start()
 
         each(32, start, 1)
 
@@ -222,19 +222,22 @@
             head(n * GROUP + k)
 
     each(NSEQ * HEADS // GROUP, group)
-    take_hidden()
 
     def tail(t):
         @pl.when(t < NJ)
         def _():
             project(1, t)
-            stage3(0, t)
 
         @pl.when((t >= 2) & (t < NJ + 2))
         def _():
             stage1(1, t - 2)
             stage1b(1, t - 2)
 
+        @pl.when(t == 3)
+        def _():
+            take_hidden()
+            each(NJ, lambda j: stage3(0, j))
+
         @pl.when((t >= 3) & (t < NJ + 3))
         def _():
             stage2(1, t - 3)
@@ -249,8 +252,8 @@
         cs[h] = dot(jnp.ones((8, 128), F32), crossp[h], NT, precision=lax.Precision.HIGHEST)
 
     def start_cross(d):
-        to = (me + d) % 16
-        send(cs.at[to // 8], cr.at[me], c_s, c_r, to_yz(to)).start()
+        to = lax.rem(me + d, 16)
+        send(cs.at[lax.div(to, 8)], cr.at[me], c_s, c_r, to_yz(to)).start()
 
     each(16, start_cross, 1)
 

time: 57.2 us -> 57.3 us (level)
  no operation moved by 1% of the time
where the time goes in v4:
time: 57.3 us; the launch traced here: 57.1 us
  Pallas kernels  55.6 us (97%)
  local copies, waits for them, and re-layouts  1.47 us (3%)
    pallas_call x1, Pallas kernels, per_device(): pl.pallas_call(kernel, out_shape=jax.ShapeDtypeStruct((NSEQ, 64, 64), F32...  55.6 us
    unnamed x1, local copies, waits for them, and re-layouts  1.47 us

profile of v4, /device:TPU:1, one launch (start us, length us, event | category | flops | bytes accessed | tf_op | source)
XLA Modules:
  0.0 57.1 jit_solution(6104445474134639826)
XLA Ops:
  0.0 55.6 %shard_map.82 = f32[2,64,64]{2,1,0:T(8,128)} custom-call(bf16[1,2,512,1024]{3,2,1,0:T(8,128)(2,1)} %q_hbm.1, bf16[1,2,512,1024]{3,2,1,0:T(8,128)(2,1)} %k_hbm.1, bf16[1,2,512,1024]{3,2,1,0:T(8,128)(2,1)} %v_hbm.1, bf16[1,2,512,1024]{3,2,1,0:T(8,128)(2,1)} %g_hbm.1, bf16[1,1024,1024]{2,1,0:T(8,128)(2,1)} %wk_hbm.1, bf16[1,1024,1024]{2,1,0:T(8,128)(2,1)} %wv_hbm.1, ...), custom_call_target="tpu_custom_call" | custom-call | tf_op jit(solution)/shard_map/pallas_call | solution.py:314
  55.6 1.5 %copy.10 = f32[2,64,64]{2,1,0:T(8,128)} copy(f32[2,64,64]{2,1,0:T(8,128)} %shard_map.82) | data formatting | bytes 65536
